TPU v7x, 32 devices: a whole 2x2x4 slice. The times are simulated.
32 devices in a mesh: spin: 2 (over x), row: 4 (over z), col: 4 (over y, core).
Axes of the slice: x: 2, y: 2, z: 4, core: 2. Of those that a mesh axis runs over, the one named last changes fastest.
Arguments:
- hamiltonian: float32 [7168, 3584], P(('spin', 'row'), 'col'), parts along dimension 0
- bounds: float32 [4], P('spin'), parts along dimension 0
- n_occ: int32 [2], P('spin'), parts along dimension 0
Outputs:
- output 1: float32 [7168, 3584], P(('spin', 'row'), 'col'), parts along dimension 0
- output 2: float32 [2], P('spin'), parts along dimension 0
There are 2 independent parts. A program takes and returns all parts, laid end to end along the dimension named above; each array names one.
All inputs are finite; a program needn't handle non-finite values.
Results may differ from a plain program's by a relative error of at most 0.001.
Values sent between devices are 32-bit elements.
A program may use at most 1 GiB of HBM per device.

v0:
```python
import jax
import jax.numpy as jnp
from jax import lax
from jax.sharding import PartitionSpec as P

STEPS = 3


def solution(mesh):
    n_cols = mesh.shape["col"]
    highest = lax.Precision.HIGHEST

    def local_fn(ham_blk, bounds, n_occ):
        rows_n, cols_n = ham_blk.shape
        mat_order = cols_n * n_cols
        row_ids = lax.axis_index("row") * rows_n + lax.broadcasted_iota(jnp.int32, (rows_n, 1), 0)
        col_ids = lax.axis_index("col") * cols_n + lax.broadcasted_iota(jnp.int32, (1, cols_n), 1)
        diag_mask = row_ids == col_ids
        occupied = n_occ[0].astype(jnp.float32)
        mu_val = lax.psum(jnp.sum(jnp.where(diag_mask, ham_blk, 0.0)), ("row", "col")) / mat_order
        lam_scale = jnp.minimum(occupied / (bounds[1] - mu_val), (mat_order - occupied) / (mu_val - bounds[0]))
        density = jnp.where(diag_mask, (lam_scale * mu_val + occupied) / mat_order, 0.0) - (lam_scale / mat_order) * ham_blk
        for _ in range(STEPS):
            x_rows = lax.all_gather(density, "col", axis=1, tiled=True)
            x_cols = lax.all_gather(density, "row", axis=0, tiled=True)
            dens_sq = jnp.dot(x_rows, x_cols, precision=highest, preferred_element_type=jnp.float32)
            sq_rows = lax.all_gather(dens_sq, "col", axis=1, tiled=True)
            dens_cube = jnp.dot(sq_rows, x_cols, precision=highest, preferred_element_type=jnp.float32)
            part_sums = jnp.stack([jnp.sum(jnp.where(diag_mask, density, 0.0)), jnp.sum(density * density), jnp.sum(dens_sq * density)])
            traces = lax.psum(part_sums, ("row", "col"))
            mix_coef = (traces[1] - traces[2]) / (traces[0] - traces[1])
            density = ((1.0 - 2.0 * mix_coef) * density + (1.0 + mix_coef) * dens_sq - dens_cube) / (1.0 - mix_coef)
        energy = 2.0 * lax.psum(jnp.sum(density * ham_blk), ("row", "col"))
        return density, energy[None]

    spec_mat = P(("spin", "row"), "col")
    return jax.shard_map(local_fn, mesh=mesh, in_specs=(spec_mat, P("spin"), P("spin")), out_specs=(spec_mat, P("spin")), check_vma=False)
```

profile of v0, /device:TPU:0, one launch (start us, length us, event | category | flops | bytes accessed | tf_op | source)
XLA Modules:
  0.0 1555.5 jit_solution(16708236845602643817)
XLA Ops:
  7.2 0.0 copy-start.1
  7.2 0.0 copy-start.5
  7.2 0.0 all-gather.12.cloned.1.call-start
  7.2 3.6 fusion
  10.8 35.6 %psum.35 = f32[]{:T(128)} all-reduce(f32[]{:T(128)} %fusion), channel_id=1, replica_groups=mesh['spin'=2,'row'=4,'col'=4] {'row','col'}, use_global_device_ids=true, to_apply=%region_1.2 | all-reduce | flops 1 | bytes 8 | tf_op jit(solution)/shard_map/psum | solution.py:20
  46.4 0.0 copy-done.5
  46.4 0.7 fusion.8
  49.7 0.0 copy-done.1
  49.7 2.1 fusion.1
  51.9 0.0 copy-start
  51.9 0.0 all-gather.12.cloned.1.call-update
  51.9 0.0 all-gather.10.cloned.1.call-start
  52.0 0.7 all-gather.10.cloned.1.call-update
  52.7 0.0 all-gather.14.cloned.1.call-start
  52.7 219.6 %all-gather.12.cloned.1.call-done = f32[3584,896]{1,0:T(8,128)} async-done(((f32[896,896]{1,0:T(8,128)}), f32[3584,896]{1,0:T(8,128)}) %all-gather.12.cloned.1.call-update) | async-done | bytes 12845072 | tf_op jit(solution)/shard_map/all_gather | solution.py:25
  272.3 84.6 %all-gather.10.cloned.1.call-done = f32[896,3584]{1,0:T(8,128)} async-done(((f32[896,896]{1,0:T(8,128)}), f32[896,3584]{1,0:T(8,128)}) %all-gather.10.cloned.1.call-update) | async-done | bytes 12845072 | tf_op jit(solution)/shard_map/all_gather | solution.py:24
  356.9 0.0 copy-done
  356.9 47.5 %fusion.2 = (f32[]{:T(128)}, f32[]{:T(128)}, f32[]{:T(128)}, f32[896,896]{1,0:T(8,128)}) fusion(f32[896,896]{1,0:T(8,128)S(1)} %copy-done, s32[896]{0:T(1024)S(1)} %get-tuple-element.27, s32[896]{0:T(1024)S(1)} %get-tuple-element.28, f32[896,3584]{1,0:T(8,128)} %all-gather.10.cloned.1.call-done, f32[3584,896]{1,0:T(8,128)} %all-gather.12.cloned.1.call-done), kind=kOutput, calls=%fused_computation.7 | convolution fusion | flops 34533130240 | bytes 32119820 | tf_op jit(solution)/shard_map/dot_general | solution.py:26
  404.4 0.0 all-gather.14.cloned.1.call-update
  404.4 0.0 all-gather.16.cloned.1.call-start
  404.5 2.0 pad_maximum_fusion
  406.4 32.8 %psum.36 = f32[3]{0:T(128)S(1)} all-reduce(f32[3]{0:T(128)S(1)} %pad_maximum_fusion), channel_id=1, replica_groups=mesh['spin'=2,'row'=4,'col'=4] {'row','col'}, use_global_device_ids=true, to_apply=%region_5.6 | all-reduce | flops 3 | bytes 24 | tf_op jit(solution)/shard_map/psum | solution.py:30
  439.3 0.6 fusion.7
  442.5 46.7 %all-gather.14.cloned.1.call-done = f32[896,3584]{1,0:T(8,128)} async-done(((f32[896,896]{1,0:T(8,128)}), f32[896,3584]{1,0:T(8,128)}) %all-gather.14.cloned.1.call-update) | async-done | bytes 12845072 | tf_op jit(solution)/shard_map/all_gather | solution.py:27
  489.3 47.5 %subtract_divide_fusion.2 = f32[896,896]{1,0:T(8,128)} fusion(f32[896,896]{1,0:T(8,128)} %get-tuple-element.22, f32[896,896]{1,0:T(8,128)S(1)} %copy-done, f32[896,3584]{1,0:T(8,128)} %all-gather.14.cloned.1.call-done, f32[3584,896]{1,0:T(8,128)} %all-gather.12.cloned.1.call-done, f32[]{:T(128)} %bitcast.8, f32[]{:T(128)} %bitcast.7, f32[]{:T(128)} %bitcast.6), kind=kOutput, calls=%fused_computation.17 | convolution fusion | flops 34531524608 | bytes 35323916 | tf_op jit(solution)/shard_map/dot_general | solution.py:28
  536.8 0.0 copy-start.4
  536.8 0.0 all-gather.16.cloned.1.call-update
  536.8 0.0 all-gather.18.cloned.1.call-start
  536.8 0.5 all-gather.18.cloned.1.call-update
  537.4 0.3 all-gather.20.cloned.1.call-start
  537.7 83.5 %all-gather.16.cloned.1.call-done = f32[896,3584]{1,0:T(8,128)} async-done(((f32[896,896]{1,0:T(8,128)}), f32[896,3584]{1,0:T(8,128)}) %all-gather.16.cloned.1.call-update) | async-done | bytes 12845072 | tf_op jit(solution)/shard_map/all_gather | solution.py:24
  621.2 225.0 %all-gather.18.cloned.1.call-done = f32[3584,896]{1,0:T(8,128)} async-done(((f32[896,896]{1,0:T(8,128)}), f32[3584,896]{1,0:T(8,128)}) %all-gather.18.cloned.1.call-update) | async-done | bytes 12845072 | tf_op jit(solution)/shard_map/all_gather | solution.py:25
  846.2 0.0 copy-done.4
  846.2 47.5 %fusion.3 = (f32[]{:T(128)}, f32[]{:T(128)}, f32[]{:T(128)}, f32[896,896]{1,0:T(8,128)}) fusion(f32[896,896]{1,0:T(8,128)S(1)} %copy-done.4, s32[896]{0:T(1024)S(1)} %get-tuple-element.27, s32[896]{0:T(1024)S(1)} %get-tuple-element.28, f32[896,3584]{1,0:T(8,128)} %all-gather.16.cloned.1.call-done, f32[3584,896]{1,0:T(8,128)} %all-gather.18.cloned.1.call-done), kind=kOutput, calls=%fused_computation.8 | convolution fusion | flops 34533130240 | bytes 32119820 | tf_op jit(solution)/shard_map/dot_general | solution.py:26
  893.7 0.0 all-gather.20.cloned.1.call-update
  893.7 0.0 all-gather.22.cloned.1.call-start
  893.7 2.0 pad_maximum_fusion.1
  895.7 30.9 %psum.37 = f32[3]{0:T(128)S(1)} all-reduce(f32[3]{0:T(128)S(1)} %pad_maximum_fusion.1), channel_id=1, replica_groups=mesh['spin'=2,'row'=4,'col'=4] {'row','col'}, use_global_device_ids=true, to_apply=%region_9.10 | all-reduce | flops 3 | bytes 24 | tf_op jit(solution)/shard_map/psum | solution.py:30
  926.6 0.6 fusion.6
  929.8 46.9 %all-gather.20.cloned.1.call-done = f32[896,3584]{1,0:T(8,128)} async-done(((f32[896,896]{1,0:T(8,128)}), f32[896,3584]{1,0:T(8,128)}) %all-gather.20.cloned.1.call-update) | async-done | bytes 12845072 | tf_op jit(solution)/shard_map/all_gather | solution.py:27
  976.7 47.5 %subtract_divide_fusion.1 = f32[896,896]{1,0:T(8,128)} fusion(f32[896,896]{1,0:T(8,128)} %get-tuple-element.23, f32[896,896]{1,0:T(8,128)S(1)} %copy-done.4, f32[896,3584]{1,0:T(8,128)} %all-gather.20.cloned.1.call-done, f32[3584,896]{1,0:T(8,128)} %all-gather.18.cloned.1.call-done, f32[]{:T(128)} %bitcast.14, f32[]{:T(128)} %bitcast.13, f32[]{:T(128)} %bitcast.12), kind=kOutput, calls=%fused_computation.14 | convolution fusion | flops 34531524608 | bytes 35323916 | tf_op jit(solution)/shard_map/dot_general | solution.py:28
  1024.2 0.0 copy-start.3
  1024.2 0.0 all-gather.22.cloned.1.call-update
  1024.2 0.0 all-gather.24.cloned.1.call-start
  1024.3 0.7 all-gather.24.cloned.1.call-update
  1025.0 0.6 all-gather.26.cloned.1.call-start
  1025.6 83.1 %all-gather.22.cloned.1.call-done = f32[896,3584]{1,0:T(8,128)} async-done(((f32[896,896]{1,0:T(8,128)}), f32[896,3584]{1,0:T(8,128)}) %all-gather.22.cloned.1.call-update) | async-done | bytes 12845072 | tf_op jit(solution)/shard_map/all_gather | solution.py:24
  1108.7 225.2 %all-gather.24.cloned.1.call-done = f32[3584,896]{1,0:T(8,128)} async-done(((f32[896,896]{1,0:T(8,128)}), f32[3584,896]{1,0:T(8,128)}) %all-gather.24.cloned.1.call-update) | async-done | bytes 12845072 | tf_op jit(solution)/shard_map/all_gather | solution.py:25
  1333.8 0.0 copy-done.3
  1333.8 47.5 %fusion.4 = (f32[]{:T(128)}, f32[]{:T(128)}, f32[]{:T(128)}, f32[896,896]{1,0:T(8,128)}) fusion(f32[896,896]{1,0:T(8,128)S(1)} %copy-done.3, s32[896]{0:T(1024)S(1)} %get-tuple-element.27, s32[896]{0:T(1024)S(1)} %get-tuple-element.28, f32[896,3584]{1,0:T(8,128)} %all-gather.22.cloned.1.call-done, f32[3584,896]{1,0:T(8,128)} %all-gather.24.cloned.1.call-done), kind=kOutput, calls=%fused_computation.9 | convolution fusion | flops 34533130240 | bytes 32119820 | tf_op jit(solution)/shard_map/dot_general | solution.py:26
  1381.3 0.0 copy-start.2
  1381.3 0.0 all-gather.26.cloned.1.call-update
  1381.3 2.2 pad_maximum_fusion.2
  1383.5 30.8 %psum.38 = f32[3]{0:T(128)S(1)} all-reduce(f32[3]{0:T(128)S(1)} %pad_maximum_fusion.2), channel_id=1, replica_groups=mesh['spin'=2,'row'=4,'col'=4] {'row','col'}, use_global_device_ids=true, to_apply=%region_13.14 | all-reduce | flops 3 | bytes 24 | tf_op jit(solution)/shard_map/psum | solution.py:30
  1414.3 0.6 fusion.5
  1417.4 47.0 %all-gather.26.cloned.1.call-done = f32[896,3584]{1,0:T(8,128)} async-done(((f32[896,896]{1,0:T(8,128)}), f32[896,3584]{1,0:T(8,128)}) %all-gather.26.cloned.1.call-update) | async-done | bytes 12845072 | tf_op jit(solution)/shard_map/all_gather | solution.py:27
  1464.3 0.0 copy-done.2
  1464.3 49.4 %multiply_reduce_fusion = (f32[]{:T(128)}, f32[896,896]{1,0:T(8,128)}) fusion(f32[896,896]{1,0:T(8,128)S(1)} %copy-done.2, f32[]{:T(128)} %bitcast.20, f32[896,3584]{1,0:T(8,128)} %all-gather.26.cloned.1.call-done, f32[3584,896]{1,0:T(8,128)} %all-gather.24.cloned.1.call-done, f32[896,896]{1,0:T(8,128)} %get-tuple-element.24, f32[]{:T(128)} %bitcast.19, ...), kind=kOutput, calls=%fused_computation.10 | convolution fusion | flops 34533130240 | bytes 38535184 | tf_op jit(solution)/shard_map/dot_general | solution.py:28
  1513.7 33.3 %psum.39 = f32[]{:T(128)} all-reduce(f32[]{:T(128)} %get-tuple-element.25), channel_id=1, replica_groups=mesh['spin'=2,'row'=4,'col'=4] {'row','col'}, use_global_device_ids=true, to_apply=%region_15.16 | all-reduce | flops 1 | bytes 8 | tf_op jit(solution)/shard_map/psum | solution.py:33
  (1 shorter events, 0.0 us)
Async XLA Ops:
  7.2 42.6 %copy-start.1 = (f32[896,896]{1,0:T(8,128)S(1)}, f32[896,896]{1,0:T(8,128)}, u32[]{:S(2)}) copy-start(f32[896,896]{1,0:T(8,128)} %param.3) | copy-start | bytes 9633796
  7.2 39.2 %copy-start.5 = (f32[2]{0:T(128)S(1)}, f32[2]{0:T(128)}, u32[]{:S(2)}) copy-start(f32[2]{0:T(128)} %param.4) | copy-start | bytes 28
  7.2 265.1 %all-gather.12.cloned.1.call-start = ((), (), s32[]{:S(2)}) async-start(), calls=%async_computation.1 | async-start | bytes 16056320 | tf_op jit(solution)/shard_map/all_gather | solution.py:25
  51.9 305.0 %copy-start = (f32[896,896]{1,0:T(8,128)S(1)}, f32[896,896]{1,0:T(8,128)}, u32[]{:S(2)}) copy-start(f32[896,896]{1,0:T(8,128)} %fusion.1) | copy-start | bytes 9633796
  51.9 305.0 %all-gather.10.cloned.1.call-start = ((), (), s32[]{:S(2)}) async-start(), calls=%async_computation | async-start | bytes 16056320 | tf_op jit(solution)/shard_map/all_gather | solution.py:24
  52.7 436.6 %all-gather.14.cloned.1.call-start = ((), (), s32[]{:S(2)}) async-start(), calls=%async_computation.2 | async-start | bytes 16056320 | tf_op jit(solution)/shard_map/all_gather | solution.py:27
  404.4 216.8 %all-gather.16.cloned.1.call-start = ((), (), s32[]{:S(2)}) async-start(), calls=%async_computation.3 | async-start | bytes 16056320 | tf_op jit(solution)/shard_map/all_gather | solution.py:24
  536.8 309.4 %copy-start.4 = (f32[896,896]{1,0:T(8,128)S(1)}, f32[896,896]{1,0:T(8,128)}, u32[]{:S(2)}) copy-start(f32[896,896]{1,0:T(8,128)} %subtract_divide_fusion.2) | copy-start | bytes 9633796
  536.8 309.4 %all-gather.18.cloned.1.call-start = ((), (), s32[]{:S(2)}) async-start(), calls=%async_computation.4 | async-start | bytes 16056320 | tf_op jit(solution)/shard_map/all_gather | solution.py:25
  537.4 439.4 %all-gather.20.cloned.1.call-start = ((), (), s32[]{:S(2)}) async-start(), calls=%async_computation.5 | async-start | bytes 16056320 | tf_op jit(solution)/shard_map/all_gather | solution.py:27
  893.7 215.0 %all-gather.22.cloned.1.call-start = ((), (), s32[]{:S(2)}) async-start(), calls=%async_computation.6 | async-start | bytes 16056320 | tf_op jit(solution)/shard_map/all_gather | solution.py:24
  1024.2 309.6 %copy-start.3 = (f32[896,896]{1,0:T(8,128)S(1)}, f32[896,896]{1,0:T(8,128)}, u32[]{:S(2)}) copy-start(f32[896,896]{1,0:T(8,128)} %subtract_divide_fusion.1) | copy-start | bytes 9633796
  1024.2 309.6 %all-gather.24.cloned.1.call-start = ((), (), s32[]{:S(2)}) async-start(), calls=%async_computation.7 | async-start | bytes 16056320 | tf_op jit(solution)/shard_map/all_gather | solution.py:25
  1025.0 439.3 %all-gather.26.cloned.1.call-start = ((), (), s32[]{:S(2)}) async-start(), calls=%async_computation.8 | async-start | bytes 16056320 | tf_op jit(solution)/shard_map/all_gather | solution.py:27
  1381.3 83.1 %copy-start.2 = (f32[896,896]{1,0:T(8,128)S(1)}, f32[896,896]{1,0:T(8,128)}, u32[]{:S(2)}) copy-start(f32[896,896]{1,0:T(8,128)} %param.3) | copy-start | bytes 9633796
Sparse Core Ops, SparseCore 0:
  52.0 220.2 all-gather.11
  274.4 82.4 all-gather.9
  404.5 84.6 all-gather.13
  536.9 84.2 all-gather.15
  623.2 222.9 all-gather.17
  893.8 82.8 all-gather.19
  1024.4 84.2 all-gather.21
  1110.8 222.9 all-gather.23
  1381.4 82.8 all-gather.25
where the time goes:
time: 1560 us
  waiting for transfers between devices  1060 us (68%)
  matrix products  287 us (18%)
  blocking collectives  163 us (10%)
  between operations  26.1 us (2%)
    all_gather x3, waiting for transfers between devices, local_fn(): x_cols = lax.all_gather(density, 'row', axis=0, tiled=True)  670 us
    all_gather x3, waiting for transfers between devices, local_fn(): x_rows = lax.all_gather(density, 'col', axis=1, tiled=True)  251 us
    dot_general x3, matrix products, local_fn(): jnp.dot(sq_rows, x_cols, precision=highest, preferred_element_type=jnp.fl...  144 us
    dot_general x3, matrix products, local_fn(): jnp.dot(x_rows, x_cols, precision=highest, preferred_element_type=jnp.flo...  142 us
    all_gather x3, waiting for transfers between devices, local_fn(): sq_rows = lax.all_gather(dens_sq, 'col', axis=1, tiled=True)  141 us
    psum x3, blocking collectives, local_fn(): traces = lax.psum(part_sums, ('row', 'col'))  94.5 us
    psum x1, blocking collectives, local_fn(): lax.psum(jnp.sum(jnp.where(diag_mask, ham_blk, 0.0)), ('row', 'col'))  35.6 us
    psum x1, blocking collectives, local_fn(): energy = 2.0 * lax.psum(jnp.sum(density * ham_blk), ('row', 'col'))  33.3 us
  transfers between devices with their start and end apart: 9, of which 9 were waited for; matrix products, arithmetic and copies ran while one was open for 1% of the time, Pallas kernels for 0%

commit v1 on v0

v1 whole, which is shorter than its diff:
```python
import functools

import jax
import jax.numpy as jnp
from jax import lax
from jax.experimental import pallas as pl
from jax.experimental.pallas import tpu as pltpu
from jax.sharding import PartitionSpec as P

STEPS = 3
GRID = 4
HIGHEST = lax.Precision.HIGHEST
MESH = pl.DeviceIdType.MESH
VMEM_BYTES = 62 * 2**20
BLOCKS = ((0, 0), (0, 1), (0, 2), (1, 1), (1, 2), (2, 2), (2, 3), (3, 3), (3, 0), (3, 1))
NB = len(BLOCKS)
EARLY = (3, 5)
ORDER = (
    (0, 1, 2, 3, 4, 5, 6, 7, 8, 9),
    (3, 4, 0, 5, 1, 6, 2, 7, 8, 9),
    (5, 6, 7, 3, 8, 4, 9, 0, 1, 2),
    (7, 8, 9, 5, 6, 3, 4, 0, 1, 2),
)
LAG = 2


def pick(index, values):
    out = jnp.int32(values[-1])
    for k in range(len(values) - 2, -1, -1):
        out = jnp.where(index == k, jnp.int32(values[k]), out)
    return out


def order_of(z, t):
    return pick(z, [0] * GRID) + sum(jnp.where(z == k, pick(t, ORDER[k]), 0) for k in range(GRID))


def block_of(i, j):
    table = [0] * (GRID * GRID)
    for b, (bi, bj) in enumerate(BLOCKS):
        table[bi * GRID + bj] = b
        table[bj * GRID + bi] = b
    stored = [1 if (k // GRID, k % GRID) in BLOCKS else 0 for k in range(GRID * GRID)]
    at = i * GRID + j
    return pick(at, table), pick(at, stored)


def remote(src, dst, send_sem, recv_sem, z, q):
    return pltpu.make_async_remote_copy(
        src_ref=src, dst_ref=dst, send_sem=send_sem, recv_sem=recv_sem, device_id={"row": z, "col": q}, device_id_type=MESH
    )


def group_barrier(z, q):
    barrier = pltpu.get_barrier_semaphore()
    me = z * GRID + q

    def signal(k, carry):
        to = (me + k) % (GRID * GRID)
        pl.semaphore_signal(barrier, inc=1, device_id={"row": to // GRID, "col": to % GRID}, device_id_type=MESH)
        return carry

    lax.fori_loop(1, GRID * GRID, signal, 0)
    pl.semaphore_wait(barrier, GRID * GRID - 1)


def reduce_copy(k, me, red, send_sems, recv_sems):
    to = (me + k) % (GRID * GRID)
    return remote(red.at[me], red.at[me], send_sems.at[k], recv_sems.at[me], to // GRID, to % GRID)


def reduce_start(me, red, send_sems, recv_sems):
    def body(k, carry):
        reduce_copy(k, me, red, send_sems, recv_sems).start()
        return carry

    lax.fori_loop(1, GRID * GRID, body, 0)


def reduce_finish(me, red, send_sems, recv_sems):
    def body(k, carry):
        frm = (me + k) % (GRID * GRID)
        remote(red.at[frm], red.at[frm], send_sems.at[k], recv_sems.at[frm], frm // GRID, frm % GRID).wait_recv()
        reduce_copy(k, me, red, send_sems, recv_sems).wait_send()
        return carry

    lax.fori_loop(1, GRID * GRID, body, 0)
    return jnp.sum(red[...], axis=0)


def as_tile(*sums):
    row = lax.broadcasted_iota(jnp.int32, (8, 128), 0)
    tile = jnp.zeros((8, 128), jnp.float32)
    for k, value in enumerate(sums):
        tile = jnp.where(row == k, value, tile)
    return tile


def prepare_kernel(order, ham, bounds, n_occ, ham_strip, dens, red, send_sem, recv_sem, red_send, red_recv):
    z, q = lax.axis_index("row"), lax.axis_index("col")
    me = z * GRID + q
    rows, cols = ham.shape[1:]
    local_row = lax.broadcasted_iota(jnp.int32, (rows, cols), 0)
    local_col = lax.broadcasted_iota(jnp.int32, (rows, cols), 1)
    group_barrier(z, q)

    def exchange(k):
        to = (q + k) % GRID
        return remote(ham.at[to], ham_strip.at[q], send_sem.at[k], recv_sem.at[q], z, to)

    for k in (2, 3, 1):
        exchange(k).start()
    part = jnp.float32(0.0)
    for s in range(GRID):
        part += jnp.sum(jnp.where((local_row + s * rows == local_col) & (z == q), ham[s], 0.0))
    red[me] = as_tile(part)
    ham_strip[q] = ham[q]
    reduce_start(me, red, red_send, red_recv)
    total = reduce_finish(me, red, red_send, red_recv)
    mu = total[0:1, 0:1] / order
    occ = n_occ[0].astype(jnp.float32)
    occ_v = jnp.full((1, 1), occ)
    low, high = jnp.full((1, 1), bounds[0]), jnp.full((1, 1), bounds[1])
    lam = jnp.minimum(occ_v / (high - mu), (order - occ_v) / (mu - low))
    scale, shift = lam / order, occ_v / order

    def write(j):
        on_diag = (local_row + q * rows == local_col) & (z == j)
        dens[j] = scale * (jnp.where(on_diag, mu, 0.0) - ham_strip[j]) + jnp.where(on_diag, shift, 0.0)

    write(q)
    for k in (1, 2, 3):
        frm = (q + k) % GRID
        remote(ham.at[0], ham_strip.at[frm], send_sem.at[k], recv_sem.at[frm], z, frm).wait_recv()
        write(frm)
    for k in (1, 2, 3):
        exchange(k).wait_send()


def step_kernel(last, *refs):
    if last:
        strip, ham_strip, out, energy, xall, sq, res, red, red2 = refs[:9]
        recv, sent, red_send, red_recv, red2_send, red2_recv, out_send, out_recv = refs[9:]
    else:
        strip, out, xall, sq, red = refs[:5]
        recv, sent, red_send, red_recv = refs[5:]
        res = out
    z, q = lax.axis_index("row"), lax.axis_index("col")
    me = z * GRID + q
    other = (q + 2) % GRID
    mate = q + 1 - 2 * (q % 2)
    mate_other = (mate + 2) % GRID
    rows, cols = strip.shape[1:]
    local_row = lax.broadcasted_iota(jnp.int32, (rows, cols), 0)
    local_col = lax.broadcasted_iota(jnp.int32, (rows, cols), 1)
    row_of = [i for i, _ in BLOCKS]
    col_of = [j for _, j in BLOCKS]

    def is_early(b):
        return functools.reduce(jnp.logical_or, [b == e for e in EARLY])

    def hop(src, b, s, line, kind, z_to, q_to):
        return remote(src, xall.at[b, s], sent.at[b, line, kind], recv.at[b, s], z_to, q_to)

    def forward(src, b, s, line, cross, act):
        origin = pick(b, row_of)

        @pl.when((z >= origin) & (z < GRID - 1) & cross[0])
        def _():
            act(hop(src, b, s, line, 0, z + 1, q))

        @pl.when((z <= origin) & (z > 0) & cross[0])
        def _():
            act(hop(src, b, s, line, 1, z - 1, q))

        if line == 0:

            @pl.when(cross[1])
            def _():
                act(hop(src, b, s, line, 2, z, other))

        act(hop(src, b, s, line, 3, z, mate))

    def arrived(b, s):
        remote(xall.at[b, s], xall.at[b, s], sent.at[b, 0, 0], recv.at[b, s], z, mate).wait_recv()

    def start(copy):
        copy.start()

    def wait_send(copy):
        copy.wait_send()

    def own_lines(t, act, waits):
        b = order_of(z, t)
        origin, col = pick(b, row_of), pick(b, col_of)
        early = is_early(b)

        @pl.when(origin == z)
        def _():
            forward(strip.at[col], b, q, 0, (True, True), act)

        @pl.when(origin != z)
        def _():
            if waits:
                arrived(b, q)
            forward(xall.at[b, q], b, q, 0, (True, jnp.logical_not(early)), act)

        @pl.when(early)
        def _():
            if waits:
                arrived(b, other)
            forward(xall.at[b, other], b, other, 1, (True, False), act)

    def late_line(b, act, waits):
        @pl.when(jnp.logical_not(is_early(b)))
        def _():
            if waits:
                arrived(b, other)
            act(hop(xall.at[b, other], b, other, 1, 3, z, mate))

    group_barrier(z, q)
    for k in range(GRID):
        sq[k] = jnp.zeros((rows, cols), jnp.float32)

    def gather(t, carry):
        @pl.when(t < NB)
        def _():
            own_lines(t, start, True)

        @pl.when(t >= LAG)
        def _():
            b = order_of(z, t - LAG)
            i, j = pick(b, row_of), pick(b, col_of)
            late_line(b, start, True)
            arrived(b, mate)
            arrived(b, mate_other)

            @pl.when(i == z)
            def _():
                xall[b, q] = strip[j]

            block = xall.at[b]
            whole = block[...].reshape(GRID * rows, cols)
            sq[j] += jnp.dot(strip[i], whole, precision=HIGHEST, preferred_element_type=jnp.float32)

            @pl.when(i != j)
            def _():
                sq[i] += lax.dot_general(
                    strip[j], whole, (((1,), (1,)), ((), ())), precision=HIGHEST, preferred_element_type=jnp.float32
                )

        return carry

    lax.fori_loop(0, NB + LAG, gather, 0)

    def sums(j, carry):
        t1, t2, t3 = carry
        x = strip[j]
        on_diag = (local_row + q * rows == local_col) & (z == j)
        return (
            t1 + jnp.sum(jnp.where(on_diag, x, 0.0)),
            t2 + jnp.sum(x * x),
            t3 + jnp.sum(sq[j] * x),
        )

    zero = jnp.float32(0.0)
    t1, t2, t3 = lax.fori_loop(0, GRID, sums, (zero, zero, zero))
    red[me] = as_tile(t1, t2, t3)
    for k in range(GRID):
        res[k] = jnp.zeros((rows, cols), jnp.float32)
    reduce_start(me, red, red_send, red_recv)

    def cube(jj, total_energy):
        j = (q + 1 + jj) % GRID

        def inner(i, carry):
            b, stored = block_of(i, j)

            @pl.when(stored == 1)
            def _():
                whole = xall[b].reshape(GRID * rows, cols)
                res[j] += jnp.dot(sq[i], whole, precision=HIGHEST, preferred_element_type=jnp.float32)

            @pl.when(stored == 0)
            def _():
                whole = xall[b].reshape(GRID * rows, cols)
                res[j] += lax.dot_general(
                    sq[i], whole, (((1,), (1,)), ((), ())), precision=HIGHEST, preferred_element_type=jnp.float32
                )

            return carry

        lax.fori_loop(0, GRID, inner, 0)

        @pl.when(jj == 0)
        def _():
            red[0] = reduce_finish(me, red, red_send, red_recv)

        total = red[0]
        s1, s2, s3 = total[0:1, 0:1], total[1:2, 0:1], total[2:3, 0:1]
        mix = (s2 - s3) / (s1 - s2)
        new = ((1.0 - 2.0 * mix) * strip[j] + (1.0 + mix) * sq[j] - res[j]) / (1.0 - mix)
        res[j] = new
        if not last:
            return total_energy
        total_energy += jnp.sum(res[j] * ham_strip[j])

        @pl.when(jj < GRID - 1)
        def _():
            remote(res.at[j], out.at[q], out_send.at[j], out_recv.at[q], z, j).start()

        @pl.when(jj == GRID - 1)
        def _():
            out[q] = res[j]

        return total_energy

    part = lax.fori_loop(0, GRID, cube, zero)

    def drain(t, carry):
        own_lines(t, wait_send, False)
        late_line(order_of(z, t), wait_send, False)
        return carry

    if last:
        red2[me] = as_tile(2.0 * part)
        lax.fori_loop(0, NB, drain, 0)
        reduce_start(me, red2, red2_send, red2_recv)
        for k in (1, 2, 3):
            j = (q + k) % GRID
            remote(res.at[j], out.at[q], out_send.at[j], out_recv.at[q], z, j).wait_send()
            remote(res.at[j], out.at[j], out_send.at[j], out_recv.at[j], z, j).wait_recv()
        energy[...] = reduce_finish(me, red2, red2_send, red2_recv)
    else:
        lax.fori_loop(0, NB, drain, 0)


def vmem_spec():
    return pl.BlockSpec(memory_space=pltpu.VMEM)


def call_params(which):
    return pltpu.CompilerParams(collective_id=which, has_side_effects=True, vmem_limit_bytes=VMEM_BYTES)


def solution(mesh):
    peers = GRID * GRID
    dma = pltpu.SemaphoreType.DMA

    def local_fn(ham_blk, bounds, n_occ):
        size, cols = ham_blk.shape
        rows = size // GRID
        order = float(cols * mesh.shape["col"])
        f32 = jnp.float32
        strip = jax.ShapeDtypeStruct((GRID, rows, cols), f32)
        smem = pl.BlockSpec(memory_space=pltpu.SMEM)
        ham_strip, dens = pl.pallas_call(
            functools.partial(prepare_kernel, order),
            out_shape=(strip, strip),
            in_specs=[vmem_spec(), smem, smem],
            out_specs=(vmem_spec(), vmem_spec()),
            scratch_shapes=[pltpu.VMEM((peers, 8, 128), f32), dma((GRID,)), dma((GRID,)), dma((peers,)), dma((peers,))],
            compiler_params=call_params(0),
            name="prepare",
        )(ham_blk.reshape(GRID, rows, cols), bounds, n_occ)
        for step in range(STEPS):
            last = step == STEPS - 1
            scratch = [pltpu.VMEM((NB, GRID, rows, cols), f32), pltpu.VMEM((GRID, rows, cols), f32)]
            sems = [dma((NB, GRID)), dma((NB, 2, 4)), dma((peers,)), dma((peers,))]
            red = pltpu.VMEM((peers, 8, 128), f32)
            if last:
                scratch += [pltpu.VMEM((GRID, rows, cols), f32), red, red]
                sems += [dma((peers,)), dma((peers,)), dma((GRID,)), dma((GRID,))]
            else:
                scratch += [red]
            result = pl.pallas_call(
                functools.partial(step_kernel, last),
                out_shape=(strip, jax.ShapeDtypeStruct((8, 128), f32)) if last else strip,
                in_specs=[vmem_spec()] * (2 if last else 1),
                out_specs=(vmem_spec(), vmem_spec()) if last else vmem_spec(),
                scratch_shapes=scratch + sems,
                compiler_params=call_params(1 + step),
                name="purify_last" if last else "purify",
            )(*((dens, ham_strip) if last else (dens,)))
            dens = result[0] if last else result
        return dens.reshape(size, cols), result[1][0, :1]

    spec_mat = P(("spin", "row"), "col")
    return jax.shard_map(
        local_fn, mesh=mesh, in_specs=(spec_mat, P("spin"), P("spin")), out_specs=(spec_mat, P("spin")), check_vma=False
    )
```

time: 1560 us -> 809 us (0.52)
  waiting for transfers between devices: 1060 us -> 0 us
  Pallas kernels: 0 us -> 796 us
  matrix products: 287 us -> 0 us
  blocking collectives: 163 us -> 0 us
  between operations: 26.1 us -> 1.81 us
    all_gather x9 -> x0, waiting for transfers between devices: 1060 us -> none  [the longest x3 670 us: local_fn(): x_cols = lax.all_gather(density, 'row', axis=0, tiled=True)]
    pallas_call x0 -> x4, Pallas kernels: none -> 796 us  [the longest x3 747 us: local_fn(): pl.pallas_call(functools.partial(step_kernel, last), out_shape=(strip, ja...]
    dot_general x6 -> x0, matrix products: 287 us -> none  [the longest x3 144 us: local_fn(): jnp.dot(sq_rows, x_cols, precision=highest, preferred_element_type=jnp.fl...]
    psum x5 -> x0, blocking collectives: 163 us -> none  [the longest x3 94.5 us: local_fn(): traces = lax.psum(part_sums, ('row', 'col'))]
  transfers between devices with their start and end apart: 9 -> 0, of which waited for: 9 -> 0; matrix products, arithmetic and copies ran while one was open for 1% -> 0% of each run, Pallas kernels for 0% -> 0%
where the time goes in v1:
time: 809 us; the launch traced here: 803 us
  Pallas kernels  796 us (98%)
    pallas_call x3, Pallas kernels, local_fn(): pl.pallas_call(functools.partial(step_kernel, last), out_shape=(strip, ja...  747 us
    pallas_call x1, Pallas kernels, local_fn(): pl.pallas_call(functools.partial(prepare_kernel, order), out_shape=(strip...  49.1 us

profile of v1, /device:TPU:0, one launch (start us, length us, event | category | flops | bytes accessed | tf_op | source)
XLA Modules:
  0.0 803.2 jit_solution(17645822105270796293)
XLA Ops:
  1.3 49.1 %prepare.1 = (f32[4,224,896]{2,1,0:T(8,128)}, f32[4,224,896]{2,1,0:T(8,128)}) custom-call(f32[4,224,896]{2,1,0:T(8,128)} %bitcast.3, f32[2]{0:T(128)} %bounds.1, s32[1]{0:T(128)S(6)} %copy.6.n_occ), custom_call_target="tpu_custom_call" | custom-call | tf_op jit(solution)/shard_map/prepare/pallas_call | solution.py:357
  50.4 245.0 %purify.2.refs_0_ = f32[4,224,896]{2,1,0:T(8,128)} custom-call(f32[4,224,896]{2,1,0:T(8,128)} %get-tuple-element.6.refs_0_), custom_call_target="tpu_custom_call" | custom-call | tf_op jit(solution)/shard_map/purify/pallas_call | solution.py:376
  295.5 247.1 %purify.3.refs_0_ = f32[4,224,896]{2,1,0:T(8,128)} custom-call(f32[4,224,896]{2,1,0:T(8,128)} %purify.2.refs_0_), custom_call_target="tpu_custom_call" | custom-call | tf_op jit(solution)/shard_map/purify/pallas_call | solution.py:376
  542.6 255.1 %purify_last.1 = (f32[4,224,896]{2,1,0:T(8,128)}, f32[8,128]{1,0:T(8,128)}) custom-call(f32[4,224,896]{2,1,0:T(8,128)} %purify.3.refs_0_, f32[4,224,896]{2,1,0:T(8,128)} %get-tuple-element.7.refs_1_), custom_call_target="tpu_custom_call" | custom-call | tf_op jit(solution)/shard_map/purify_last/pallas_call | solution.py:376
  797.7 1.2 slice.3
  798.9 3.8 copy.7

commit v2 on v0

v2 whole, which is shorter than its diff:
```python
import functools

import jax
import jax.numpy as jnp
from jax import lax
from jax.experimental import pallas as pl
from jax.experimental.pallas import tpu as pltpu
from jax.sharding import PartitionSpec as P

STEPS = 3
GRID = 4
PEERS = GRID * GRID
HIGHEST = lax.Precision.HIGHEST
MESH = pl.DeviceIdType.MESH
VMEM_BYTES = 67043328
BLOCKS = ((0, 0), (0, 1), (0, 2), (1, 1), (1, 2), (2, 2), (2, 3), (3, 3), (3, 0), (3, 1))
NB = len(BLOCKS)
ROW_OF = tuple(i for i, _ in BLOCKS)
COL_OF = tuple(j for _, j in BLOCKS)
HALVES = 2
UNITS = HALVES * NB
UNIT_ROW = tuple(ROW_OF[u // HALVES] for u in range(UNITS))
UNIT_COL = tuple(COL_OF[u // HALVES] for u in range(UNITS))
EARLY = (5, 10, 19)
ORDER = (
    (3, 8, 13, 2, 5, 0, 17, 12, 16, 9, 4, 7, 1, 6, 19, 18, 10, 11, 14, 15),
    (0, 13, 2, 9, 16, 17, 4, 12, 10, 3, 5, 19, 6, 18, 11, 8, 14, 1, 15, 7),
    (13, 6, 16, 11, 17, 10, 8, 0, 19, 9, 12, 3, 2, 18, 7, 5, 14, 4, 15, 1),
    (14, 6, 16, 19, 13, 17, 12, 15, 8, 18, 9, 3, 2, 7, 10, 0, 11, 5, 4, 1),
)
WHOLE = tuple(tuple(int(any(row[k] // HALVES == u // HALVES for k in range(t))) for t, u in enumerate(row)) for row in ORDER)
PLACE = (
    (0, 1, 2, 3, 4, 5, 6, 7, 8, 9),
    (2, 4, 6, 0, 1, 3, 5, 7, 8, 9),
    (7, 8, 9, 3, 5, 0, 1, 2, 4, 6),
    (7, 8, 9, 5, 6, 3, 4, 0, 1, 2),
)
FIRST = (0, 3, 5, 7)
COUNT = (3, 2, 2, 3)
COLUMNS = ((0, 1, 2, 3), (1, 2, 0, 3), (2, 3, 0, 1), (3, 0, 1, 2))
SLOTS = 16
LAND, SPARE = (2 * NB + NB) % SLOTS, (2 * NB + NB + 1) % SLOTS
LAG = 5
PARTS = ((0, 512), (512, 896))


def pick(index, values):
    out = jnp.int32(values[-1])
    for k in range(len(values) - 2, -1, -1):
        out = jnp.where(index == k, jnp.int32(values[k]), out)
    return out


def pick2(row, col, table):
    return pick(row * len(table[0]) + col, [v for line in table for v in line])


def slot_of(step, z, b):
    return (NB * step + pick2(z, b, PLACE)) % SLOTS


def block_of(i, j):
    table = [0] * PEERS
    for b, (bi, bj) in enumerate(BLOCKS):
        table[bi * GRID + bj] = b
        table[bj * GRID + bi] = b
    stored = [1 if (k // GRID, k % GRID) in BLOCKS else 0 for k in range(PEERS)]
    at = i * GRID + j
    return pick(at, table), pick(at, stored)


def remote(src, dst, send_sem, recv_sem, z, q):
    return pltpu.make_async_remote_copy(
        src_ref=src, dst_ref=dst, send_sem=send_sem, recv_sem=recv_sem, device_id={"row": z, "col": q}, device_id_type=MESH
    )


def group_barrier(me):
    barrier = pltpu.get_barrier_semaphore()

    def signal(k, carry):
        to = (me + k) % PEERS
        pl.semaphore_signal(barrier, inc=1, device_id={"row": to // GRID, "col": to % GRID}, device_id_type=MESH)
        return carry

    lax.fori_loop(1, PEERS, signal, 0)
    pl.semaphore_wait(barrier, PEERS - 1)


def reduce_copy(k, me, red, send_sems, recv_sems):
    to = (me + k) % PEERS
    return remote(red.at[me], red.at[me], send_sems.at[k], recv_sems.at[me], to // GRID, to % GRID)


def reduce_start(me, red, send_sems, recv_sems):
    def body(k, carry):
        reduce_copy(k, me, red, send_sems, recv_sems).start()
        return carry

    lax.fori_loop(1, PEERS, body, 0)


def reduce_finish(me, red, send_sems, recv_sems):
    def body(k, carry):
        frm = (me + k) % PEERS
        remote(red.at[frm], red.at[frm], send_sems.at[k], recv_sems.at[frm], frm // GRID, frm % GRID).wait_recv()
        reduce_copy(k, me, red, send_sems, recv_sems).wait_send()
        return carry

    lax.fori_loop(1, PEERS, body, 0)
    return jnp.sum(red[...], axis=0)


def as_tile(*sums):
    row = lax.broadcasted_iota(jnp.int32, (8, 128), 0)
    tile = jnp.zeros((8, 128), jnp.float32)
    for k, value in enumerate(sums):
        tile = jnp.where(row == k, value, tile)
    return tile


def purify_kernel(
    order, ham, bounds, n_occ, out, energy, xall, strip, sq, acc, red, red2, total,
    recv, sent, red_send, red_recv, red2_send, red2_recv, ex_send, ex_recv, out_send, out_recv, local_sem, credit,
):
    z, q = lax.axis_index("row"), lax.axis_index("col")
    me = z * GRID + q
    other = (q + 2) % GRID
    mate = q + 1 - 2 * (q % 2)
    mate_other = (mate + 2) % GRID
    rows, cols = strip.shape[1:]
    local_row = lax.broadcasted_iota(jnp.int32, (rows, cols), 0)
    local_col = lax.broadcasted_iota(jnp.int32, (rows, cols), 1)

    def on_diag(j):
        return (local_row + q * rows == local_col) & (z == j)

    half = rows // HALVES

    def part_of(s):
        return pl.ds(pl.multiple_of(s * rows, 8), rows)

    def piece_of(slot, s):
        return xall.at[slot, part_of(s)]

    def unit_at(step, z_at, u, s):
        at = pl.ds(pl.multiple_of(s * rows + (u % HALVES) * half, 8), half)
        return xall.at[slot_of(step, z_at, u // HALVES), at]

    def add_product(out, lhs, slot):
        for lo, hi in PARTS:
            out[:, lo:hi] += jnp.dot(lhs[...], xall[slot, :, lo:hi], precision=HIGHEST, preferred_element_type=jnp.float32)

    def add_mirrored(out, lhs, slot):
        for lo, hi in PARTS:
            out[:, lo:hi] += lax.dot_general(
                lhs[...], xall[slot, lo:hi, :], (((1,), (1,)), ((), ())), precision=HIGHEST, preferred_element_type=jnp.float32
            )

    def is_early(u):
        return functools.reduce(jnp.logical_or, [u == e for e in EARLY])

    def hop(step, src, u, s, line, kind, z_to, q_to):
        return remote(src, unit_at(step, z_to, u, s), sent.at[u, line, kind], recv.at[u, s], z_to, q_to)

    def along(step, src, u, s, line, act):
        origin = pick(u, UNIT_ROW)

        @pl.when((z >= origin) & (z < GRID - 1))
        def _():
            act(hop(step, src, u, s, line, 0, z + 1, q))

        @pl.when((z <= origin) & (z > 0))
        def _():
            act(hop(step, src, u, s, line, 1, z - 1, q))

    def across(step, src, u, s, act):
        act(hop(step, src, u, s, 0, 2, z, other))

    def to_mate(step, src, u, s, line, act):
        act(hop(step, src, u, s, line, 3, z, mate))

    def arrived(step, u, s):
        unit = unit_at(step, z, u, s)
        remote(unit, unit, sent.at[u, 0, 0], recv.at[u, s], z, mate).wait_recv()

    def start(copy):
        copy.start()

    def wait_send(copy):
        copy.wait_send()

    def own_unit(step, n, act):
        u = HALVES * pick(z, FIRST) + n
        src = strip.at[pick(u, UNIT_COL), pl.ds(pl.multiple_of((u % HALVES) * half, 8), half)]
        along(step, src, u, q, 0, act)
        across(step, src, u, q, act)
        to_mate(step, src, u, q, 0, act)

    def publish(step, jj):
        b = pick(z, FIRST) + jj
        xall[slot_of(step, z, b), part_of(q)] = strip[pick(b, COL_OF)]
        for h in range(HALVES):
            own_unit(step, HALVES * jj + h, start)

    def relay(step, t, act, waits):
        u = pick2(z, t, ORDER)
        early = is_early(u)

        @pl.when(pick(u, UNIT_ROW) != z)
        def _():
            if waits:
                arrived(step, u, q)
            src = unit_at(step, z, u, q)
            along(step, src, u, q, 0, act)

            @pl.when(jnp.logical_not(early))
            def _():
                across(step, src, u, q, act)

            to_mate(step, src, u, q, 0, act)

        @pl.when(early)
        def _():
            if waits:
                arrived(step, u, other)
            src = unit_at(step, z, u, other)
            along(step, src, u, other, 1, act)
            to_mate(step, src, u, other, 1, act)

    def late(step, u, act, waits):
        @pl.when(jnp.logical_not(is_early(u)))
        def _():
            if waits:
                arrived(step, u, other)
            to_mate(step, unit_at(step, z, u, other), u, other, 1, act)

    group_barrier(me)

    def exchange(k):
        to = (q + k) % GRID
        return remote(ham.at[part_of(to)], strip.at[q], ex_send.at[k], ex_recv.at[q], z, to)

    for k in (2, 3, 1):
        exchange(k).start()
    load = pltpu.make_async_copy(ham, xall.at[SPARE], local_sem)
    load.start()
    load.wait()
    part = jnp.float32(0.0)
    for s in range(GRID):
        part += jnp.sum(jnp.where((local_row + s * rows == local_col) & (z == q), xall[SPARE, s * rows : (s + 1) * rows], 0.0))
    red[me] = as_tile(part)
    strip[q] = xall[SPARE, part_of(q)]
    reduce_start(me, red, red_send, red_recv)
    mu = reduce_finish(me, red, red_send, red_recv)[0:1, 0:1] / order
    occ = jnp.full((1, 1), n_occ[0].astype(jnp.float32))
    low, high = jnp.full((1, 1), bounds[0]), jnp.full((1, 1), bounds[1])
    lam = jnp.minimum(occ / (high - mu), (order - occ) / (mu - low))
    scale, shift = lam / order, occ / order

    def initial(jj, carry):
        j = pick2(z, jj, COLUMNS)

        @pl.when(j != q)
        def _():
            remote(ham.at[part_of(0)], strip.at[j], ex_send.at[0], ex_recv.at[j], z, j).wait_recv()

        strip[j] = scale * (jnp.where(on_diag(j), mu, 0.0) - strip[j]) + jnp.where(on_diag(j), shift, 0.0)

        @pl.when(jj < pick(z, COUNT))
        def _():
            publish(0, jj)

        return carry

    lax.fori_loop(0, GRID, initial, 0)
    for k in (1, 2, 3):
        exchange(k).wait_send()

    def one_step(step, carry):
        last = step == STEPS - 1
        for k in range(GRID):
            sq[k] = jnp.zeros((rows, cols), jnp.float32)

        def gather(t, carry):
            @pl.when(t < UNITS)
            def _():
                relay(step, t, start, True)

            @pl.when(t >= LAG)
            def _():
                u = pick2(z, t - LAG, ORDER)
                i, j = pick(u, UNIT_ROW), pick(u, UNIT_COL)
                late(step, u, start, True)
                arrived(step, u, mate)
                arrived(step, u, mate_other)
                whole = pick2(z, t - LAG, WHOLE) == 1
                slot = slot_of(step, z, u // HALVES)

                @pl.when(whole)
                def _():
                    add_product(sq.at[j], strip.at[i], slot)

                @pl.when(whole & (i != j))
                def _():
                    add_mirrored(sq.at[i], strip.at[j], slot)

            return carry

        lax.fori_loop(0, UNITS + LAG, gather, 0)

        def sums(j, carry):
            t1, t2, t3 = carry
            x = strip[j]
            return (
                t1 + jnp.sum(jnp.where(on_diag(j), x, 0.0)),
                t2 + jnp.sum(x * x),
                t3 + jnp.sum(sq[j] * x),
            )

        zero = jnp.float32(0.0)
        red[me] = as_tile(*lax.fori_loop(0, GRID, sums, (zero, zero, zero)))
        acc[...] = jnp.zeros((rows, cols), jnp.float32)
        reduce_start(me, red, red_send, red_recv)

        def cube(jj, carry):
            j = jnp.where(last, (q + 1 + jj) % GRID, pick2(z, jj, COLUMNS))

            def inner(i, carry):
                b, stored = block_of(i, j)
                slot = slot_of(step, z, b)

                @pl.when(stored == 1)
                def _():
                    add_product(acc, sq.at[i], slot)

                @pl.when(stored == 0)
                def _():
                    add_mirrored(acc, sq.at[i], slot)

                return carry

            lax.fori_loop(0, GRID, inner, 0)

            @pl.when(jj == 0)
            def _():
                def drain(t, carry):
                    @pl.when(t < HALVES * pick(z, COUNT))
                    def _():
                        own_unit(step, t, wait_send)

                    relay(step, t, wait_send, False)
                    late(step, pick2(z, t, ORDER), wait_send, False)
                    return carry

                lax.fori_loop(0, UNITS, drain, 0)
                total[...] = reduce_finish(me, red, red_send, red_recv)

            sums_v = total[...]
            s1, s2, s3 = sums_v[0:1, 0:1], sums_v[1:2, 0:1], sums_v[2:3, 0:1]
            mix = (s2 - s3) / (s1 - s2)
            strip[j] = ((1.0 - 2.0 * mix) * strip[j] + (1.0 + mix) * sq[j] - acc[...]) / (1.0 - mix)
            acc[...] = jnp.zeros((rows, cols), jnp.float32)

            @pl.when(jnp.logical_not(last) & (jj < 2))
            def _():
                publish(step + 1, jj)

            @pl.when(last & (jj < GRID - 1))
            def _():
                remote(strip.at[j], piece_of(LAND, q), out_send.at[j], out_recv.at[q], z, j).start()

            @pl.when(last & (jj == GRID - 1))
            def _():
                xall[LAND, part_of(q)] = strip[j]

            return carry

        @pl.when(last)
        def _():
            pltpu.make_async_copy(ham, xall.at[SPARE], local_sem).start()

        lax.fori_loop(0, GRID, cube, 0)

        @pl.when(jnp.logical_not(last))
        def _():
            @pl.when(z < GRID - 1)
            def _():
                pl.semaphore_signal(credit, inc=1, device_id={"row": z + 1, "col": q}, device_id_type=MESH)

            @pl.when(z > 0)
            def _():
                pl.semaphore_signal(credit, inc=1, device_id={"row": z - 1, "col": q}, device_id_type=MESH)

            pl.semaphore_signal(credit, inc=1, device_id={"row": z, "col": other}, device_id_type=MESH)
            pl.semaphore_signal(credit, inc=1, device_id={"row": z, "col": mate}, device_id_type=MESH)
            pl.semaphore_wait(credit, pick(z, (3, 4, 4, 3)))

            @pl.when(pick(z, COUNT) == 3)
            def _():
                publish(step + 1, 2)

        return carry

    lax.fori_loop(0, STEPS, one_step, 0)

    pltpu.make_async_copy(ham, xall.at[SPARE], local_sem).wait()
    for k in (1, 2, 3):
        j = (q + k) % GRID
        remote(strip.at[j], piece_of(LAND, q), out_send.at[j], out_recv.at[q], z, j).wait_send()
        remote(strip.at[j], piece_of(LAND, j), out_send.at[j], out_recv.at[j], z, j).wait_recv()
    store = pltpu.make_async_copy(xall.at[LAND], out, local_sem)
    store.start()
    part = jnp.float32(0.0)
    for s in range(GRID):
        part += jnp.sum(xall[LAND, s * rows : (s + 1) * rows] * xall[SPARE, s * rows : (s + 1) * rows])
    red2[me] = as_tile(2.0 * part)
    store.wait()
    reduce_start(me, red2, red2_send, red2_recv)
    energy[...] = reduce_finish(me, red2, red2_send, red2_recv)


def solution(mesh):
    def local_fn(ham_blk, bounds, n_occ):
        size, cols = ham_blk.shape
        rows = size // GRID
        order = float(cols * mesh.shape["col"])
        f32 = jnp.float32
        dma = pltpu.SemaphoreType.DMA
        strip = (GRID, rows, cols)
        smem = pl.BlockSpec(memory_space=pltpu.SMEM)
        anywhere = pl.BlockSpec(memory_space=pl.ANY)
        red = pltpu.VMEM((PEERS, 8, 128), f32)
        density, energy = pl.pallas_call(
            functools.partial(purify_kernel, order),
            out_shape=(jax.ShapeDtypeStruct((size, cols), f32), jax.ShapeDtypeStruct((8, 128), f32)),
            in_specs=[anywhere, smem, smem],
            out_specs=(anywhere, pl.BlockSpec(memory_space=pltpu.VMEM)),
            scratch_shapes=[
                pltpu.VMEM((SLOTS, size, cols), f32),
                pltpu.VMEM(strip, f32),
                pltpu.VMEM(strip, f32),
                pltpu.VMEM((rows, cols), f32),
                red,
                red,
                pltpu.VMEM((8, 128), f32),
                dma((UNITS, GRID)),
                dma((UNITS, 2, 4)),
                dma((PEERS,)),
                dma((PEERS,)),
                dma((PEERS,)),
                dma((PEERS,)),
                dma((GRID,)),
                dma((GRID,)),
                dma((GRID,)),
                dma((GRID,)),
                dma,
                pltpu.SemaphoreType.REGULAR,
            ],
            compiler_params=pltpu.CompilerParams(collective_id=0, has_side_effects=True, vmem_limit_bytes=VMEM_BYTES),
            name="purify",
        )(ham_blk, bounds, n_occ)
        return density, energy[0, :1]

    spec_mat = P(("spin", "row"), "col")
    return jax.shard_map(
        local_fn, mesh=mesh, in_specs=(spec_mat, P("spin"), P("spin")), out_specs=(spec_mat, P("spin")), check_vma=False
    )
```

time: 1560 us -> 651 us (0.42)
  waiting for transfers between devices: 1060 us -> 0 us
  Pallas kernels: 0 us -> 644 us
  matrix products: 287 us -> 0 us
  blocking collectives: 163 us -> 0 us
  between operations: 26.1 us -> 1.28 us
    all_gather x9 -> x0, waiting for transfers between devices: 1060 us -> none  [the longest x3 670 us: local_fn(): x_cols = lax.all_gather(density, 'row', axis=0, tiled=True)]
    pallas_call x0 -> x1, Pallas kernels: none -> 644 us  [local_fn(): pl.pallas_call(functools.partial(purify_kernel, order), out_shape=(jax.Sh...]
    dot_general x6 -> x0, matrix products: 287 us -> none  [the longest x3 144 us: local_fn(): jnp.dot(sq_rows, x_cols, precision=highest, preferred_element_type=jnp.fl...]
    psum x5 -> x0, blocking collectives: 163 us -> none  [the longest x3 94.5 us: local_fn(): traces = lax.psum(part_sums, ('row', 'col'))]
  transfers between devices with their start and end apart: 9 -> 0, of which waited for: 9 -> 0; matrix products, arithmetic and copies ran while one was open for 1% -> 0% of each run, Pallas kernels for 0% -> 0%
where the time goes in v2:
time: 651 us; the launch traced here: 650 us
  Pallas kernels  644 us (99%)
    pallas_call x1, Pallas kernels, local_fn(): pl.pallas_call(functools.partial(purify_kernel, order), out_shape=(jax.Sh...  644 us

profile of v2, /device:TPU:0, one launch (start us, length us, event | category | flops | bytes accessed | tf_op | source)
XLA Modules:
  0.0 650.4 jit_solution(2003205748805123117)
XLA Ops:
  1.3 644.1 %purify.1 = (f32[896,896]{1,0:T(8,128)}, f32[8,128]{1,0:T(8,128)}) custom-call(f32[896,896]{1,0:T(8,128)} %ham.1, f32[2]{0:T(128)} %bounds.1, s32[1]{0:T(128)S(6)} %copy.6.n_occ), custom_call_target="tpu_custom_call" | custom-call | tf_op jit(solution)/shard_map/purify/pallas_call | solution.py:434
  645.4 1.2 slice.3
  646.6 3.8 copy.7

commit v3 on v2

--- a/solution.py
+++ b/solution.py
@@ -40,7 +40,7 @@
 COLUMNS = ((0, 1, 2, 3), (1, 2, 0, 3), (2, 3, 0, 1), (3, 0, 1, 2))
 SLOTS = 16
 LAND, SPARE = (2 * NB + NB) % SLOTS, (2 * NB + NB + 1) % SLOTS
-LAG = 5
+LAG, DOT_LAG = 5, 6
 PARTS = ((0, 512), (512, 896))
 
 
@@ -287,14 +287,17 @@
             def _():
                 relay(step, t, start, True)
 
-            @pl.when(t >= LAG)
-            def _():
-                u = pick2(z, t - LAG, ORDER)
+            @pl.when((t >= LAG) & (t < UNITS + LAG))
+            def _():
+                late(step, pick2(z, t - LAG, ORDER), start, True)
+
+            @pl.when(t >= DOT_LAG)
+            def _():
+                u = pick2(z, t - DOT_LAG, ORDER)
                 i, j = pick(u, UNIT_ROW), pick(u, UNIT_COL)
-                late(step, u, start, True)
                 arrived(step, u, mate)
                 arrived(step, u, mate_other)
-                whole = pick2(z, t - LAG, WHOLE) == 1
+                whole = pick2(z, t - DOT_LAG, WHOLE) == 1
                 slot = slot_of(step, z, u // HALVES)
 
                 @pl.when(whole)
@@ -307,7 +310,7 @@
 
             return carry
 
-        lax.fori_loop(0, UNITS + LAG, gather, 0)
+        lax.fori_loop(0, UNITS + DOT_LAG, gather, 0)
 
         def sums(j, carry):
             t1, t2, t3 = carry

time: 651 us -> 661 us (1.015)
  Pallas kernels: 644 us -> 655 us
    pallas_call x1, Pallas kernels: 644 us -> 655 us  [local_fn(): pl.pallas_call(functools.partial(purify_kernel, order), out_shape=(jax.Sh...]
where the time goes in v3:
time: 661 us
  Pallas kernels  655 us (99%)
    pallas_call x1, Pallas kernels, local_fn(): pl.pallas_call(functools.partial(purify_kernel, order), out_shape=(jax.Sh...  655 us

profile of v3, /device:TPU:0, one launch (start us, length us, event | category | flops | bytes accessed | tf_op | source)
XLA Modules:
  0.0 660.9 jit_solution(18158552583507561325)
XLA Ops:
  1.3 654.6 %purify.1 = (f32[896,896]{1,0:T(8,128)}, f32[8,128]{1,0:T(8,128)}) custom-call(f32[896,896]{1,0:T(8,128)} %ham.1, f32[2]{0:T(128)} %bounds.1, s32[1]{0:T(128)S(6)} %copy.6.n_occ), custom_call_target="tpu_custom_call" | custom-call | tf_op jit(solution)/shard_map/purify/pallas_call | solution.py:437
  655.9 1.2 slice.3
  657.1 3.8 copy.7
